TPU v7x, 512 devices: a whole 4x4x16 slice. The times are simulated.
512 devices in a mesh: dp: 32 (over z_lo, x), tensor: 16 (over z_hi, y, core).
Axes of the slice: x: 4, y: 4, z: 16 (z_hi: 2, z_lo: 8; z = z_hi * 8 + z_lo), core: 2. Of those that a mesh axis runs over, the one named last changes fastest.
Arguments:
- hidden: bfloat16 [8192, 14336], P('dp', 'tensor'), parts along dimension 0, may hold values from -16 to 16
- signs: int32 [14336], P('tensor'), may hold values 0 or 1
- packed: int32 [14336, 512], P('tensor'), may hold values from -2147483648 to 2147483646
- group_scales: int32 [112, 4096], P('tensor'), may hold values from 1 to 16
- residual: bfloat16 [8192, 4096], P(('dp', 'tensor')), parts along dimension 0, may hold values from -16 to 16
Outputs:
- new_residual: bfloat16 [8192, 4096], P(('dp', 'tensor')), parts along dimension 0
- normed: bfloat16 [8192, 4096], P(('dp', 'tensor')), parts along dimension 0
There are 32 independent parts, one for each index of `dp`. A program takes and returns all parts, laid end to end along the dimension named above; an argument that names none is the same for every part. Nothing has to cross between parts.
Inputs may be any that keep to these rules, and one draw needn't show every extreme that they name: `packed`: bits 4 k to 4 k + 3 of word j in row f hold the code of output feature k * 512 + j plus 8.
All inputs are finite; a program needn't handle non-finite values. No bound on the sum of `signs` on one device may be relied on, other than what follows from the above.
Results may differ from a plain program's by a relative error of at most 0.0054.
Values may be sent and summed in bfloat16 or wider, within the bound.
A program may use at most 64 MiB of HBM per device.

v0:
```python
import math

import jax
import jax.numpy as jnp
import numpy as np
from jax import lax
from jax.sharding import Mesh
from jax.sharding import PartitionSpec as P

FF = 14336
TENSOR = ("tensor_0", "tensor_1", "tensor_2")
DP_TENSOR = ("dp", "tensor_0", "tensor_1", "tensor_2")


def in_blocks(shard, dim, length):
    dims = shard.shape
    blocks = shard.reshape(*dims[:dim], length, dims[dim] // length, *dims[dim + 1 :])
    return jnp.moveaxis(blocks, dim, 0)


def sum_at_owner(shard, axis, dim):
    length = lax.axis_size(axis)
    blocks = lax.all_to_all(in_blocks(shard, dim, length), axis, 0, 0, tiled=True)
    return jnp.sum(blocks, axis=0)


def sum_in_two_steps(shard, axes, dim):
    far, near = axes
    blocks = in_blocks(shard, dim, lax.axis_size(far))
    nearer = sum_at_owner(blocks, near, dim + 1)
    arrived = lax.all_to_all(nearer, far, split_axis=0, concat_axis=0, tiled=True)
    return arrived.sum(axis=0)


def paley_table():
    offsets = (np.arange(13)[None, :] - np.arange(13)[:, None]) % 13
    residues = np.zeros(13)
    residues[np.arange(1, 13) ** 2 % 13] = 1.0
    quadratic = np.where(offsets == 0, 0.0, np.where(residues[offsets] > 0, 1.0, -1.0))
    conference = np.zeros((14, 14))
    conference[0, 1:] = 1.0
    conference[1:, 0] = 1.0
    conference[1:, 1:] = quadratic
    upper = np.array([[1.0, 1.0], [1.0, -1.0]])
    lower = np.array([[1.0, -1.0], [-1.0, -1.0]])
    return np.kron(conference, upper) + np.kron(np.eye(14), lower)


def sylvester(order):
    first = lax.broadcasted_iota(jnp.int32, (order, order), 0)
    second = lax.broadcasted_iota(jnp.int32, (order, order), 1)
    common = first & second
    parity = jnp.zeros((order, order), jnp.int32)
    for bit in range(max(order.bit_length() - 1, 0)):
        parity = parity ^ jnp.right_shift(common, bit) & 1
    return (1 - 2 * parity).astype(jnp.float32)


def dequantize(packed, group_scales, local_width):
    word_cols = packed.shape[1]
    group_count = group_scales.shape[0]
    group_size = local_width // group_count
    pieces = []
    for nibble in range(8):
        codes = (jnp.right_shift(packed, 4 * nibble) & 15) - 8
        scales = group_scales[:, nibble * word_cols : (nibble + 1) * word_cols]
        weights = codes.reshape(group_count, group_size, word_cols) * scales[:, None, :]
        pieces.append(weights.reshape(local_width, word_cols).astype(jnp.bfloat16))
    return jnp.concatenate(pieces, axis=1)


def local(hidden, signs, packed, group_scales, residual):
    groups = lax.axis_size(TENSOR)
    local_width = hidden.shape[1]
    inner = jnp.asarray(paley_table(), jnp.float32)
    outer = sylvester(local_width // 28)
    table = (
        (outer[:, None, :, None] * inner[None, :, None, :])
        .reshape(local_width, local_width)
        .astype(jnp.bfloat16)
    )
    flips = (2 * signs - 1).astype(jnp.bfloat16)
    signed = hidden * flips[None, :]
    partial_rot = jnp.dot(signed, table, preferred_element_type=jnp.float32)
    unit = 1.0 / math.sqrt(FF)
    spread = lax.all_to_all(partial_rot, TENSOR, split_axis=0, concat_axis=1, tiled=True)
    token_rows = spread.shape[0]
    stacked = spread.reshape(token_rows, groups, local_width)
    mixed = jnp.einsum("rpw,qp->rqw", stacked, sylvester(groups), precision=lax.Precision.HIGHEST)
    folded = (mixed * unit).astype(jnp.bfloat16).reshape(token_rows, groups * local_width)
    rotated = lax.all_to_all(folded, TENSOR, split_axis=1, concat_axis=0, tiled=True)
    weights = dequantize(packed, group_scales, local_width)
    summed = sum_in_two_steps(
        jnp.dot(rotated, weights, preferred_element_type=jnp.float32),
        (("tensor_0", "tensor_1"), "tensor_2"),
        0,
    )
    branch = summed * (1.0 / (45.0 * math.sqrt(FF)))
    new_residual = (residual.astype(jnp.float32) + branch).astype(jnp.bfloat16)
    values = new_residual.astype(jnp.float32)
    normed = values * lax.rsqrt(jnp.mean(values * values, axis=1, keepdims=True) + 1e-05)
    return (new_residual, normed.astype(jnp.bfloat16))


def solution(mesh):
    finer = Mesh(
        mesh.devices.reshape(mesh.shape["dp"], 2, 4, 2), ("dp", "tensor_0", "tensor_1", "tensor_2")
    )
    in_specs = (P("dp", TENSOR), P(TENSOR), P(TENSOR, None), P(TENSOR, None), P(DP_TENSOR, None))
    out_specs = (P(DP_TENSOR, None), P(DP_TENSOR, None))
    return jax.shard_map(local, mesh=finer, in_specs=in_specs, out_specs=out_specs, check_vma=False)
```

profile of v0, /device:TPU:38, one launch (start us, length us, event | category | flops | bytes accessed | tf_op | source)
XLA Modules:
  0.0 230.2 jit_solution(8672511882057523334)
XLA Ops:
  0.7 5.5 %multiply_convert_fusion = bf16[32,28,32,28]{3,2,1,0:T(8,128)(2,1)} fusion(f32[28,28]{1,0:T(8,128)} %constant.56.clone, f32[32,32]{1,0:T(8,128)S(1)} %subtract_convert_fusion), kind=kLoop, calls=%fused_computation | loop fusion | flops 1605632 | bytes 1612864 | tf_op jit(solution)/shard_map/convert_element_type | solution.py:80
  6.1 13.6 %reshape.96 = bf16[896,896,1]{1,0,2:T(8,128)(2,1)S(1)} reshape(bf16[32,28,32,28]{3,2,1,0:T(8,128)(2,1)} %multiply_convert_fusion) | data formatting | bytes 3211264 | tf_op jit(solution)/shard_map/convert_element_type | solution.py:80
  19.8 0.7 fusion.46
  20.5 70.3 %all_to_all.36 = f32[16,16,896]{2,1,0:T(8,128)S(1)} all-to-all(f32[16,16,896]{2,1,0:T(8,128)S(1)} %fusion.46), channel_id=1, replica_groups=mesh['dp'=32,'tensor_0'=2,'tensor_1'=4,'tensor_2'=2] {'tensor_0','tensor..., dimensions={0} | all-to-all | bytes 1835008 | tf_op jit(solution)/shard_map/all_to_all | solution.py:86
  90.8 1.1 fusion.14
  91.9 0.9 copy.18
  92.8 3.6 %all-to-all-start.1 = ((bf16[16,16,896]{2,0,1:T(8,128)(2,1)}), bf16[16,16,896]{2,0,1:T(8,128)(2,1)S(1)}, u32[]{:S(2)}, u32[]{:S(2)}) async-start(bf16[16,16,896]{2,0,1:T(8,128)(2,1)} %copy.18), calls=%async_computation.1 | async-start | bytes 917504 | tf_op jit(solution)/shard_map/all_to_all | solution.py:91
  96.4 2.6 %fusion.5 = (bf16[896,512]{1,0:T(8,128)(2,1)S(1)}, bf16[896,512]{1,0:T(8,128)(2,1)S(1)}, bf16[896,512]{1,0:T(8,128)(2,1)S(1)}, bf16[896,512]{1,0:T(8,128)(2,1)S(...) fusion(s32[896,512]{1,0:T(8,128)S(1)} %copy-done, ...), kind=kLoop, calls=%fused_computation.5 | loop fusion | flops 18350080 | bytes 9289728 | tf_op jit(solution)/shard_map/convert_element_type | solution.py:68
  98.9 1.1 constant_dynamic-update-slice_fusion.7
  100.0 1.0 constant_dynamic-update-slice_fusion.6
  101.1 1.1 constant_dynamic-update-slice_fusion.5
  102.1 1.1 constant_dynamic-update-slice_fusion.4
  103.2 1.1 constant_dynamic-update-slice_fusion.3
  104.3 1.1 constant_dynamic-update-slice_fusion.2
  105.4 1.1 constant_dynamic-update-slice_fusion.1
  106.5 1.1 constant_dynamic-update-slice_fusion
  107.6 7.6 %all-to-all-done.1 = bf16[16,16,896]{2,0,1:T(8,128)(2,1)S(1)} async-done(((bf16[16,16,896]{2,0,1:T(8,128)(2,1)}), bf16[16,16,896]{2,0,1:T(8,128)(2,1)S(1)}, u32[]{:S(2)}, u32[]{:S(2)}) %all-to-all-start.1) | async-done | bytes 458784 | tf_op jit(solution)/shard_map/all_to_all | solution.py:91
  115.1 5.4 %fusion.2 = f32[2,8,16,4096]{3,2,0,1:T(8,128)S(1)} fusion(bf16[8,2,16,896]{3,2,1,0:T(8,128)(2,1)S(1)} %bitcast.58, bf16[896,4096]{1,0:T(8,128)(2,1)} %constant_dynamic-update-slice_fusion), kind=kOutput, calls=%fused_computation.3 | convolution fusion | flops 1879048192 | bytes 11993088 | tf_op jit(solution)/shard_map/dot_general | solution.py:94
  120.6 0.4 copy.19
  121.0 8.2 %all_to_all.37 = f32[2,8,16,4096]{3,2,1,0:T(8,128)} all-to-all(f32[2,8,16,4096]{3,2,1,0:T(8,128)S(1)} %copy.19), channel_id=1, replica_groups=mesh['dp'=32,'tensor_0'=2,'tensor_1'=4,'tensor_2'=2] {'tensor_2'}, dimensions={0} | all-to-all | bytes 8388608 | tf_op jit(solution)/shard_map/all_to_all | solution.py:23
  129.2 2.7 %reduce_sum.27 = f32[8,16,4096]{2,1,0:T(8,128)S(1)} reduce(f32[2,8,16,4096]{3,2,1,0:T(8,128)} %all_to_all.37, f32[]{:T(128)} %constant.52.clone.1), dimensions={0}, to_apply=%region_0.0 | reduce | flops 524288 | bytes 6291460 | tf_op jit(solution)/shard_map/reduce_sum | solution.py:24
  131.8 95.6 %all_to_all.38 = f32[8,16,4096]{2,1,0:T(8,128)} all-to-all(f32[8,16,4096]{2,1,0:T(8,128)S(1)} %reduce_sum.27), channel_id=1, replica_groups=mesh['dp'=32,'tensor_0'=2,'tensor_1'=4,'tensor_2'=2] {'tensor_0','tensor..., dimensions={0} | all-to-all | bytes 4194304 | tf_op jit(solution)/shard_map/all_to_all | solution.py:31
  227.5 1.8 reduce_sum.28
  229.4 0.7 fusion.18
  (18 shorter events, 0.3 us)
Async XLA Ops:
  6.1 13.6 %copy-start.5 = (s32[896]{0:T(1024)S(1)}, s32[896]{0:T(1024)}, u32[]{:S(2)}) copy-start(s32[896]{0:T(1024)} %param.7) | copy-start | bytes 10756
  6.1 13.7 %copy-start.2 = (bf16[256,896]{1,0:T(8,128)(2,1)S(1)}, bf16[256,896]{1,0:T(8,128)(2,1)}, u32[]{:S(2)}) copy-start(bf16[256,896]{1,0:T(8,128)(2,1)} %param.6) | copy-start | bytes 1376260
  90.8 5.5 %copy-start.4 = (s32[7,4096]{1,0:T(8,128)S(1)}, s32[7,4096]{1,0:T(8,128)}, u32[]{:S(2)}) copy-start(s32[7,4096]{1,0:T(8,128)} %param.9) | copy-start | bytes 344068
  90.8 5.6 %copy-start = (s32[896,512]{1,0:T(8,128)S(1)}, s32[896,512]{1,0:T(8,128)}, u32[]{:S(2)}) copy-start(s32[896,512]{1,0:T(8,128)} %param.8) | copy-start | bytes 5505028
  92.8 22.4 %all-to-all-start.1 = ((bf16[16,16,896]{2,0,1:T(8,128)(2,1)}), bf16[16,16,896]{2,0,1:T(8,128)(2,1)S(1)}, u32[]{:S(2)}, u32[]{:S(2)}) async-start(bf16[16,16,896]{2,0,1:T(8,128)(2,1)} %copy.18), calls=%async_computation.1 | async-start | bytes 917504 | tf_op jit(solution)/shard_map/all_to_all | solution.py:91
  227.5 1.8 copy-start.3
  229.4 0.8 copy-start.1
where the time goes:
time: 231 us; the launch traced here: 230 us
  blocking collectives  174 us (75%)
  local copies, waits for them, and re-layouts  23.6 us (10%)
  other arithmetic  13.4 us (6%)
  waiting for transfers between devices  7.57 us (3%)
  matrix products  7.19 us (3%)
  starting transfers between devices  3.56 us (2%)
    all_to_all x1, blocking collectives, sum_in_two_steps(): lax.all_to_all(nearer, far, split_axis=0, concat_axis=0, tiled=True)  95.6 us
    all_to_all x1, blocking collectives, local(): lax.all_to_all(partial_rot, TENSOR, split_axis=0, concat_axis=1, tiled=True)  70.3 us
    convert_element_type x1, local copies, waits for them, and re-layouts, local(): table = (outer[:, None, :, None] * inner[None, :, None, :]).reshape(local...  13.6 us
    all_to_all x1, blocking collectives, sum_at_owner(): lax.all_to_all(in_blocks(shard, dim, length), axis, 0, 0, tiled=True)  8.16 us
    unnamed x19, local copies, waits for them, and re-layouts  7.6 us
    all_to_all x1, waiting for transfers between devices, local(): lax.all_to_all(folded, TENSOR, split_axis=1, concat_axis=0, tiled=True)  7.57 us
    convert_element_type x1, other arithmetic, local(): table = (outer[:, None, :, None] * inner[None, :, None, :]).reshape(local...  5.47 us
    dot_general x1, matrix products, local(): jnp.dot(rotated, weights, preferred_element_type=jnp.float32)  5.41 us
  transfers between devices with their start and end apart: 1, of which 1 were waited for; matrix products, arithmetic and copies ran while one was open for 5% of the time, Pallas kernels for 0%

commit v1 on v0

v1 whole, which is shorter than its diff:
```python
import functools
import math

import jax
import jax.numpy as jnp
import numpy as np
from jax import lax
from jax.experimental import pallas as pl
from jax.experimental.pallas import tpu as pltpu
from jax.sharding import PartitionSpec as P

FF = 14336
D = 4096
LOCAL = 896
WORDS = 512
GROUPS = 7
CHUNKS = 4
BLOCKS = 4
COLS = D // BLOCKS
MESH = pl.DeviceIdType.MESH
UNIT = 1.0 / math.sqrt(FF)
BRANCH = 1.0 / (45.0 * math.sqrt(FF))
F32 = jnp.float32
BF16 = jnp.bfloat16


def paley_table():
    offsets = (np.arange(13)[None, :] - np.arange(13)[:, None]) % 13
    residues = np.zeros(13)
    residues[np.arange(1, 13) ** 2 % 13] = 1.0
    quadratic = np.where(offsets == 0, 0.0, np.where(residues[offsets] > 0, 1.0, -1.0))
    conference = np.zeros((14, 14))
    conference[0, 1:] = 1.0
    conference[1:, 0] = 1.0
    conference[1:, 1:] = quadratic
    upper = np.array([[1.0, 1.0], [1.0, -1.0]])
    lower = np.array([[1.0, -1.0], [-1.0, -1.0]])
    return np.kron(conference, upper) + np.kron(np.eye(14), lower)


def sylvester(order):
    table = np.ones((1, 1))
    while table.shape[0] < order:
        table = np.kron(np.array([[1.0, 1.0], [1.0, -1.0]]), table)
    return table


def sign_of(bits):
    odd = lax.rem(bits + bits // 2, 2)
    return 1.0 - 2.0 * odd.astype(F32)


def kernel(
    hidden,
    signs,
    packed,
    scales,
    residual,
    table_hbm,
    new_out,
    norm_out,
    h,
    zin,
    sg,
    pk,
    sc,
    res,
    table,
    wts,
    v,
    vr,
    w,
    wr,
    p,
    pr,
    q,
    qr,
    r1,
    r1r,
    acc,
    local_sem,
    zin_s,
    zin_r,
    sg_s,
    sg_r,
    v_s,
    v_r,
    w_s,
    w_r,
    p_s,
    p_r,
    q_s,
    q_r,
    o_s,
    o_r,
):
    dp = lax.axis_index("dp")
    t = lax.axis_index("tensor")
    z = t // 8
    y = lax.rem(t // 2, 4)
    c = lax.rem(t, 2)

    def dev(zz, yy, cc):
        return (dp, zz * 8 + yy * 2 + cc)

    far = dev(1 - z, y, c)
    twin = dev(z, y, 1 - c)
    ring = [dev(z, lax.rem(y + d, 4), c) for d in (1, 2, 3)]

    loads = [
        pltpu.make_async_copy(hidden, h, local_sem.at[0]),
        pltpu.make_async_copy(signs, sg.at[0], local_sem.at[1]),
        pltpu.make_async_copy(packed, pk, local_sem.at[2]),
        pltpu.make_async_copy(scales, sc, local_sem.at[3]),
        pltpu.make_async_copy(table_hbm, table, local_sem.at[4]),
        pltpu.make_async_copy(residual, res, local_sem.at[5]),
    ]
    for load in loads:
        load.start()

    barrier = pltpu.get_barrier_semaphore()
    for peer in [far, twin] + ring:
        pl.semaphore_signal(barrier, 1, device_id=peer, device_id_type=MESH)
    pl.semaphore_wait(barrier, 5)

    def remote(src, dst, ss, rs, peer):
        return pltpu.make_async_remote_copy(
            src_ref=src, dst_ref=dst, send_sem=ss, recv_sem=rs, device_id=peer, device_id_type=MESH
        )

    loads[1].wait()
    sg_copy = remote(sg.at[0], sg.at[1], sg_s, sg_r, far)
    sg_copy.start()
    loads[0].wait()
    zin_copies = []
    for k in range(CHUNKS):
        half = z if k < 2 else 1 - z
        copy = remote(h.at[half, :, :, k % 2], zin.at[k], zin_s.at[k], zin_r.at[k], far)
        copy.start()
        zin_copies.append(copy)

    loads[2].wait()
    loads[3].wait()

    def dequantize(i, carry):
        rows = pl.ds(pl.multiple_of(i * 16, 16), 16)
        words = pk[rows, :] ^ jnp.int32(-2004318072)
        for k in range(8):
            codes = jnp.right_shift(jnp.left_shift(words, 28 - 4 * k), 28)
            scale = sc[pl.ds(i // 8, 1), k * WORDS : (k + 1) * WORDS]
            value = (codes.astype(F32) * scale.astype(F32)).astype(BF16)
            wts[k // 2, rows, (k % 2) * WORDS : (k % 2 + 1) * WORDS] = value
        return carry

    lax.fori_loop(0, LOCAL // 16, dequantize, 0)
    loads[4].wait()

    sg_copy.wait()
    flips = (2 * sg[...] - 1).astype(F32)
    own_flip = flips[0] * (1 - 2 * z).astype(F32)
    far_flip = flips[1]

    v_copies, w_copies, p_copies, q_copies, o_copies = {}, {}, {}, {}, {}

    def combine_far(k):
        half = 1 - z if k < 2 else z
        zin_copies[k].wait_recv()
        for g in range(GROUPS):
            lanes = slice(g * 128, (g + 1) * 128)
            own = h[half, :, :, k % 2, :, lanes].astype(F32)
            other = zin[k, :, :, :, lanes].astype(F32)
            v[k, :, :, :, lanes] = own * own_flip[g : g + 1] + other * far_flip[g : g + 1]
        v_copies[k] = remote(v.at[k], vr.at[k], v_s.at[k], v_r.at[k], twin)
        v_copies[k].start()

    def combine_twin(k):
        v_copies[k].wait_recv()
        w[k] = (vr[k] + v[k] * (1 - 2 * c).astype(F32)).astype(BF16)
        for d in range(3):
            w_copies[k, d] = remote(w.at[k], wr.at[k, d], w_s.at[k, d], w_r.at[k, d], ring[d])
            w_copies[k, d].start()

    def p_copy(k, j):
        return remote(p.at[k, j, :, 1 - c], pr.at[k, j], p_s.at[k, j], p_r.at[k, j], twin)

    def q_copy(k, j, d):
        return remote(
            q.at[k, j, lax.rem(y + d + 1, 4)], qr.at[k, j, d], q_s.at[k, j, d], q_r.at[k, j, d], ring[d]
        )

    def multiply(k):
        for d in range(3):
            w_copies[k, d].wait_recv()
        u = w[k].astype(F32) * sign_of(y)
        for d in range(3):
            source = lax.rem(y + 3 - d, 4)
            u = u + wr[k, d].astype(F32) * sign_of(y & source)
        u = u.reshape(64, LOCAL).astype(BF16)
        rotated = (jnp.dot(u, table[...], preferred_element_type=F32) * UNIT).astype(BF16)

        def block(j, carry):
            @pl.when(j < BLOCKS)
            def _():
                part = jnp.dot(rotated, wts[j], preferred_element_type=F32)
                p[k, j] = part.reshape(4, 2, 8, COLS)
                p_copy(k, j).start()

            @pl.when(j > 0)
            def _():
                i = j - 1
                p_copy(k, i).wait_recv()
                q[k, i] = (p[k, i, :, c] + pr[k, i]).astype(BF16)
                for d in range(3):
                    q_copy(k, i, d).start()

            return carry

        lax.fori_loop(0, BLOCKS + 1, block, 0)

    def o_copy(k, j):
        return remote(r1.at[k, j], r1r.at[k, j], o_s.at[k, j], o_r.at[k, j], far)

    def gather(k):
        def block(j, carry):
            total = p[k, j, y, c] + pr[k, j, y]
            for d in range(3):
                q_copy(k, j, d).wait_recv()
                total = total + qr[k, j, d].astype(F32)
            if k < 2:
                r1[k, j] = total.astype(BF16)
                o_copy(k, j).start()
            else:
                o_copy(k - 2, j).wait_recv()
                acc[k - 2, j] = total + r1r[k - 2, j].astype(F32)
            return carry

        lax.fori_loop(0, BLOCKS, block, 0)

    def finish(s):
        square = jnp.zeros((8, 1), F32)
        for j in range(BLOCKS):
            lanes = slice(j * COLS, (j + 1) * COLS)
            new = (res[s, :, lanes].astype(F32) + acc[s, j] * BRANCH).astype(BF16)
            new_out[s, :, lanes] = new
            values = new.astype(F32)
            square = square + jnp.sum(values * values, axis=1, keepdims=True)
        factor = lax.rsqrt(square * (1.0 / D) + 1e-05)
        for j in range(BLOCKS):
            lanes = slice(j * COLS, (j + 1) * COLS)
            norm_out[s, :, lanes] = (new_out[s, :, lanes].astype(F32) * factor).astype(BF16)

    combine_far(0)
    combine_twin(0)
    multiply(0)
    combine_far(1)
    combine_twin(1)
    gather(0)
    multiply(1)
    combine_far(2)
    combine_twin(2)
    gather(1)
    multiply(2)
    combine_far(3)
    combine_twin(3)
    loads[5].wait()
    gather(2)
    finish(0)
    multiply(3)
    gather(3)
    finish(1)

    for k in range(CHUNKS):
        zin_copies[k].wait_send()
        v_copies[k].wait_send()
        for d in range(3):
            w_copies[k, d].wait_send()

    def drain(j, carry):
        for k in range(CHUNKS):
            p_copy(k, j).wait_send()
            for d in range(3):
                q_copy(k, j, d).wait_send()
            if k < 2:
                o_copy(k, j).wait_send()
        return carry

    lax.fori_loop(0, BLOCKS, drain, 0)


def local(hidden, signs, packed, group_scales, residual):
    table = jnp.asarray(np.kron(sylvester(LOCAL // 28), paley_table()), BF16)
    sem = pltpu.SemaphoreType.DMA
    outs = pl.pallas_call(
        kernel,
        out_shape=[jax.ShapeDtypeStruct((2, 8, D), BF16)] * 2,
        in_specs=[pl.BlockSpec(memory_space=pl.ANY)] * 6,
        out_specs=[pl.BlockSpec(memory_space=pltpu.VMEM)] * 2,
        scratch_shapes=[
            pltpu.VMEM((2, 4, 2, 2, 8, LOCAL), BF16),
            pltpu.VMEM((CHUNKS, 4, 2, 8, LOCAL), BF16),
            pltpu.VMEM((2, GROUPS, 128), jnp.int32),
            pltpu.VMEM((LOCAL, WORDS), jnp.int32),
            pltpu.VMEM((GROUPS, D), jnp.int32),
            pltpu.VMEM((2, 8, D), BF16),
            pltpu.VMEM((LOCAL, LOCAL), BF16),
            pltpu.VMEM((BLOCKS, LOCAL, COLS), BF16),
            pltpu.VMEM((CHUNKS, 4, 2, 8, LOCAL), F32),
            pltpu.VMEM((CHUNKS, 4, 2, 8, LOCAL), F32),
            pltpu.VMEM((CHUNKS, 4, 2, 8, LOCAL), BF16),
            pltpu.VMEM((CHUNKS, 3, 4, 2, 8, LOCAL), BF16),
            pltpu.VMEM((CHUNKS, BLOCKS, 4, 2, 8, COLS), F32),
            pltpu.VMEM((CHUNKS, BLOCKS, 4, 8, COLS), F32),
            pltpu.VMEM((CHUNKS, BLOCKS, 4, 8, COLS), BF16),
            pltpu.VMEM((CHUNKS, BLOCKS, 3, 8, COLS), BF16),
            pltpu.VMEM((2, BLOCKS, 8, COLS), BF16),
            pltpu.VMEM((2, BLOCKS, 8, COLS), BF16),
            pltpu.VMEM((2, BLOCKS, 8, COLS), F32),
            sem((6,)),
            sem((CHUNKS,)),
            sem((CHUNKS,)),
            sem,
            sem,
            sem((CHUNKS,)),
            sem((CHUNKS,)),
            sem((CHUNKS, 3)),
            sem((CHUNKS, 3)),
            sem((CHUNKS, BLOCKS)),
            sem((CHUNKS, BLOCKS)),
            sem((CHUNKS, BLOCKS, 3)),
            sem((CHUNKS, BLOCKS, 3)),
            sem((2, BLOCKS)),
            sem((2, BLOCKS)),
        ],
        compiler_params=pltpu.CompilerParams(
            collective_id=0, has_side_effects=True, vmem_limit_bytes=56 * 2**20
        ),
        name="rotated_down",
    )(
        hidden.reshape(2, 4, 2, 2, 8, LOCAL),
        signs.reshape(GROUPS, 128),
        packed,
        group_scales,
        residual.reshape(2, 8, D),
        table,
    )
    return tuple(out.reshape(16, D) for out in outs)


def solution(mesh):
    in_specs = (P("dp", "tensor"), P("tensor"), P("tensor", None), P("tensor", None), P(("dp", "tensor"), None))
    out_specs = (P(("dp", "tensor"), None), P(("dp", "tensor"), None))
    return jax.shard_map(local, mesh=mesh, in_specs=in_specs, out_specs=out_specs, check_vma=False)
```

time: 231 us -> 107 us (0.46)
  the two profiles are of different devices: /device:TPU:38 before, /device:TPU:82 now
where the time goes in v1:
time: 107 us
  Pallas kernels  104 us (97%)
  local copies, waits for them, and re-layouts  3.14 us (3%)
    pallas_call x1, Pallas kernels, local(): pl.pallas_call(kernel, out_shape=[jax.ShapeDtypeStruct((2, 8, D), BF16)]...  104 us
    unnamed x2, local copies, waits for them, and re-layouts  3.14 us

profile of v1, /device:TPU:82, one launch (start us, length us, event | category | flops | bytes accessed | tf_op | source)
XLA Modules:
  0.0 107.3 jit_solution(256071391372334763)
XLA Ops:
  0.6 103.5 %rotated_down.1 = (bf16[2,8,4096]{2,1,0:T(8,128)(2,1)}, bf16[2,8,4096]{2,1,0:T(8,128)(2,1)}) custom-call(bf16[2,4,2,2,8,896]{5,4,3,2,1,0:T(8,128)(2,1)} %bitcast.5, s32[7,128]{1,0:T(8,128)} %bitcast.9, s32[896,512]{1,0:T(8,128)} %packed.1, s32[7,4096]{1,0:T(8,128)} %scales.1, bf16[2,8,4096]{2,1,0:T(8,128)(2,1)} %bitcast.6, ...), custom_call_target="tpu_custom_call" | custom-call | tf_op jit(solution)/shard_map/rotated_down/pallas_call | solution.py:293
  104.2 1.6 %copy.10 = bf16[16,4096]{1,0:T(8,128)(2,1)} copy(bf16[16,4096]{1,0:T(8,128)(2,1)} %bitcast.8) | data formatting | bytes 262144
  105.7 1.6 %copy.11 = bf16[16,4096]{1,0:T(8,128)(2,1)} copy(bf16[16,4096]{1,0:T(8,128)(2,1)} %bitcast.7) | data formatting | bytes 262144

commit v2 on v1

--- a/solution.py
+++ b/solution.py
@@ -136,7 +136,8 @@
     for k in range(CHUNKS):
         half = z if k < 2 else 1 - z
         copy = remote(h.at[half, :, :, k % 2], zin.at[k], zin_s.at[k], zin_r.at[k], far)
-        copy.start()
+        if k < 2:
+            copy.start()
         zin_copies.append(copy)
 
     loads[2].wait()
@@ -165,6 +166,8 @@
     def combine_far(k):
         half = 1 - z if k < 2 else z
         zin_copies[k].wait_recv()
+        if k + 2 < CHUNKS:
+            zin_copies[k + 2].start()
         for g in range(GROUPS):
             lanes = slice(g * 128, (g + 1) * 128)
             own = h[half, :, :, k % 2, :, lanes].astype(F32)
@@ -188,7 +191,13 @@
             q.at[k, j, lax.rem(y + d + 1, 4)], qr.at[k, j, d], q_s.at[k, j, d], q_r.at[k, j, d], ring[d]
         )
 
-    def multiply(k):
+    def pass_on(k, i):
+        p_copy(k, i).wait_recv()
+        q[k, i] = (p[k, i, :, c] + pr[k, i]).astype(BF16)
+        for d in range(3):
+            q_copy(k, i, d).start()
+
+    def multiply(k, inline=0):
         for d in range(3):
             w_copies[k, d].wait_recv()
         u = w[k].astype(F32) * sign_of(y)
@@ -205,17 +214,22 @@
                 p[k, j] = part.reshape(4, 2, 8, COLS)
                 p_copy(k, j).start()
 
-            @pl.when(j > 0)
-            def _():
-                i = j - 1
-                p_copy(k, i).wait_recv()
-                q[k, i] = (p[k, i, :, c] + pr[k, i]).astype(BF16)
-                for d in range(3):
-                    q_copy(k, i, d).start()
+            if inline:
+
+                @pl.when(j > 0)
+                def _():
+                    pass_on(k, j - 1)
 
             return carry
 
-        lax.fori_loop(0, BLOCKS + 1, block, 0)
+        lax.fori_loop(0, BLOCKS + inline, block, 0)
+
+    def reduce(k):
+        def block(j, carry):
+            pass_on(k, j)
+            return carry
+
+        lax.fori_loop(0, BLOCKS, block, 0)
 
     def o_copy(k, j):
         return remote(r1.at[k, j], r1r.at[k, j], o_s.at[k, j], o_r.at[k, j], far)
@@ -251,21 +265,24 @@
 
     combine_far(0)
     combine_twin(0)
-    multiply(0)
     combine_far(1)
     combine_twin(1)
-    gather(0)
-    multiply(1)
+    multiply(0)
+    reduce(0)
     combine_far(2)
     combine_twin(2)
+    multiply(1)
+    reduce(1)
+    gather(0)
+    combine_far(3)
+    combine_twin(3)
     gather(1)
     multiply(2)
-    combine_far(3)
-    combine_twin(3)
+    reduce(2)
+    multiply(3, 1)
     loads[5].wait()
     gather(2)
     finish(0)
-    multiply(3)
     gather(3)
     finish(1)
 
@@ -293,7 +310,7 @@
     outs = pl.pallas_call(
         kernel,
         out_shape=[jax.ShapeDtypeStruct((2, 8, D), BF16)] * 2,
-        in_specs=[pl.BlockSpec(memory_space=pl.ANY)] * 6,
+        in_specs=[pl.BlockSpec(memory_space=pltpu.HBM)] * 6,
         out_specs=[pl.BlockSpec(memory_space=pltpu.VMEM)] * 2,
         scratch_shapes=[
             pltpu.VMEM((2, 4, 2, 2, 8, LOCAL), BF16),
@@ -332,7 +349,7 @@
             sem((2, BLOCKS)),
         ],
         compiler_params=pltpu.CompilerParams(
-            collective_id=0, has_side_effects=True, vmem_limit_bytes=56 * 2**20
+            collective_id=0, has_side_effects=True, vmem_limit_bytes=66500000
         ),
         name="rotated_down",
     )(

time: 107 us -> 86 us (0.80)
  the two profiles are of different devices: /device:TPU:82 before, /device:TPU:71 now
where the time goes in v2:
time: 86 us; the launch traced here: 85.8 us
  Pallas kernels  82 us (95%)
  local copies, waits for them, and re-layouts  3.14 us (4%)
    pallas_call x1, Pallas kernels, local(): pl.pallas_call(kernel, out_shape=[jax.ShapeDtypeStruct((2, 8, D), BF16)]...  82 us
    unnamed x2, local copies, waits for them, and re-layouts  3.14 us

profile of v2, /device:TPU:71, one launch (start us, length us, event | category | flops | bytes accessed | tf_op | source)
XLA Modules:
  0.0 85.8 jit_solution(4950885360638283985)
XLA Ops:
  0.6 82.0 %rotated_down.1 = (bf16[2,8,4096]{2,1,0:T(8,128)(2,1)}, bf16[2,8,4096]{2,1,0:T(8,128)(2,1)}) custom-call(bf16[2,4,2,2,8,896]{5,4,3,2,1,0:T(8,128)(2,1)} %bitcast.5, s32[7,128]{1,0:T(8,128)} %bitcast.9, s32[896,512]{1,0:T(8,128)} %packed.1, s32[7,4096]{1,0:T(8,128)} %scales.1, bf16[2,8,4096]{2,1,0:T(8,128)(2,1)} %bitcast.6, ...), custom_call_target="tpu_custom_call" | custom-call | tf_op jit(solution)/shard_map/rotated_down/pallas_call | solution.py:310
  82.7 1.6 %copy.10 = bf16[16,4096]{1,0:T(8,128)(2,1)} copy(bf16[16,4096]{1,0:T(8,128)(2,1)} %bitcast.8) | data formatting | bytes 262144
  84.2 1.6 %copy.11 = bf16[16,4096]{1,0:T(8,128)(2,1)} copy(bf16[16,4096]{1,0:T(8,128)(2,1)} %bitcast.7) | data formatting | bytes 262144

commit v3 on v2

--- a/solution.py
+++ b/solution.py
@@ -71,6 +71,8 @@
     vr,
     w,
     wr,
+    half_rot,
+    half_send,
     p,
     pr,
     q,
@@ -115,33 +117,16 @@
         pltpu.make_async_copy(table_hbm, table, local_sem.at[4]),
         pltpu.make_async_copy(residual, res, local_sem.at[5]),
     ]
-    for load in loads:
-        load.start()
-
     barrier = pltpu.get_barrier_semaphore()
     for peer in [far, twin] + ring:
         pl.semaphore_signal(barrier, 1, device_id=peer, device_id_type=MESH)
-    pl.semaphore_wait(barrier, 5)
+    for load in loads:
+        load.start()
 
     def remote(src, dst, ss, rs, peer):
         return pltpu.make_async_remote_copy(
             src_ref=src, dst_ref=dst, send_sem=ss, recv_sem=rs, device_id=peer, device_id_type=MESH
         )
-
-    loads[1].wait()
-    sg_copy = remote(sg.at[0], sg.at[1], sg_s, sg_r, far)
-    sg_copy.start()
-    loads[0].wait()
-    zin_copies = []
-    for k in range(CHUNKS):
-        half = z if k < 2 else 1 - z
-        copy = remote(h.at[half, :, :, k % 2], zin.at[k], zin_s.at[k], zin_r.at[k], far)
-        if k < 2:
-            copy.start()
-        zin_copies.append(copy)
-
-    loads[2].wait()
-    loads[3].wait()
 
     def dequantize(i, carry):
         rows = pl.ds(pl.multiple_of(i * 16, 16), 16)
@@ -153,35 +138,81 @@
             wts[k // 2, rows, (k % 2) * WORDS : (k % 2 + 1) * WORDS] = value
         return carry
 
-    lax.fori_loop(0, LOCAL // 16, dequantize, 0)
-    loads[4].wait()
-
-    sg_copy.wait()
-    flips = (2 * sg[...] - 1).astype(F32)
-    own_flip = flips[0] * (1 - 2 * z).astype(F32)
-    far_flip = flips[1]
-
-    v_copies, w_copies, p_copies, q_copies, o_copies = {}, {}, {}, {}, {}
-
-    def combine_far(k):
-        half = 1 - z if k < 2 else z
+    loads[1].wait()
+    loads[0].wait()
+    own_flip = (2 * sg[0] - 1).astype(F32)
+    for half in range(2):
+        for s in range(2):
+            for g in range(GROUPS):
+                lanes = slice(g * 128, (g + 1) * 128)
+                own = h[half, :, :, s, :, lanes].astype(F32)
+                v[half * 2 + s, :, :, :, lanes] = (own * own_flip[g : g + 1]).astype(BF16)
+    loads[2].wait()
+    loads[3].wait()
+
+    @pl.when(z == 0)
+    def _():
+        lax.fori_loop(0, LOCAL // 16, dequantize, 0)
+
+    pl.semaphore_wait(barrier, 5)
+
+    sg_copy = remote(sg.at[0], sg.at[1], sg_s, sg_r, far)
+    sg_copy.start()
+    zin_copies = [
+        remote(
+            h.at[z, :, :, 0] if k == 0 else half_send.at[k - 1], zin.at[k], zin_s.at[k], zin_r.at[k], far
+        )
+        for k in range(CHUNKS)
+    ]
+    zin_copies[0].start()
+
+    sets = [z * 2 + 1, (1 - z) * 2, (1 - z) * 2 + 1, z * 2]
+    v_copies, w_copies = {}, {}
+    for i in range(5):
+        source = v.at[sets[i]] if i < 4 else v.at[4]
+        v_copies[i] = remote(source, vr.at[i], v_s.at[i], v_r.at[i], twin)
+        for d in range(3):
+            w_copies[i, d] = remote(w.at[i], wr.at[i, d], w_s.at[i, d], w_r.at[i, d], ring[d])
+    for i in range(4):
+        v_copies[i].start()
+
+    def spread(i):
+        v_copies[i].wait_recv()
+        own = v[sets[i]] if i < 4 else v[4]
+        twin_sign = (1 - 2 * c).astype(F32)
+        w[i] = (vr[i].astype(F32) + own.astype(F32) * twin_sign).astype(BF16)
+        for d in range(3):
+            w_copies[i, d].start()
+
+    def absorb(i):
+        for d in range(3):
+            w_copies[i, d].wait_recv()
+        u = w[i].astype(F32) * sign_of(y)
+        for d in range(3):
+            source = lax.rem(y + 3 - d, 4)
+            u = u + wr[i, d].astype(F32) * sign_of(y & source)
+        u = u.reshape(64, LOCAL).astype(BF16)
+        return jnp.dot(u, table[...], preferred_element_type=F32)
+
+    def rotate(i):
+        mine = absorb(i)
+        half_rot[sets[i]] = mine
+        if i < 3:
+            half_send[i] = mine.astype(BF16).reshape(4, 2, 8, LOCAL)
+
+    def receive(k):
         zin_copies[k].wait_recv()
         if k + 2 < CHUNKS:
             zin_copies[k + 2].start()
+
+    def spread_far():
+        sg_copy.wait()
+        far_flip = (2 * sg[1] - 1).astype(F32)
         for g in range(GROUPS):
             lanes = slice(g * 128, (g + 1) * 128)
-            own = h[half, :, :, k % 2, :, lanes].astype(F32)
-            other = zin[k, :, :, :, lanes].astype(F32)
-            v[k, :, :, :, lanes] = own * own_flip[g : g + 1] + other * far_flip[g : g + 1]
-        v_copies[k] = remote(v.at[k], vr.at[k], v_s.at[k], v_r.at[k], twin)
-        v_copies[k].start()
-
-    def combine_twin(k):
-        v_copies[k].wait_recv()
-        w[k] = (vr[k] + v[k] * (1 - 2 * c).astype(F32)).astype(BF16)
-        for d in range(3):
-            w_copies[k, d] = remote(w.at[k], wr.at[k, d], w_s.at[k, d], w_r.at[k, d], ring[d])
-            w_copies[k, d].start()
+            other = zin[0, :, :, :, lanes].astype(F32)
+            v[4, :, :, :, lanes] = (other * far_flip[g : g + 1]).astype(BF16)
+        v_copies[4].start()
 
     def p_copy(k, j):
         return remote(p.at[k, j, :, 1 - c], pr.at[k, j], p_s.at[k, j], p_r.at[k, j], twin)
@@ -191,48 +222,32 @@
             q.at[k, j, lax.rem(y + d + 1, 4)], qr.at[k, j, d], q_s.at[k, j, d], q_r.at[k, j, d], ring[d]
         )
 
-    def pass_on(k, i):
-        p_copy(k, i).wait_recv()
-        q[k, i] = (p[k, i, :, c] + pr[k, i]).astype(BF16)
-        for d in range(3):
-            q_copy(k, i, d).start()
-
-    def multiply(k, inline=0):
-        for d in range(3):
-            w_copies[k, d].wait_recv()
-        u = w[k].astype(F32) * sign_of(y)
-        for d in range(3):
-            source = lax.rem(y + 3 - d, 4)
-            u = u + wr[k, d].astype(F32) * sign_of(y & source)
-        u = u.reshape(64, LOCAL).astype(BF16)
-        rotated = (jnp.dot(u, table[...], preferred_element_type=F32) * UNIT).astype(BF16)
+    def o_copy(k, j):
+        return remote(r1.at[k, j], r1r.at[k, j], o_s.at[k, j], o_r.at[k, j], far)
+
+    def multiply(k):
+        far_part = absorb(4) if k == 0 else zin[k].astype(F32).reshape(64, LOCAL)
+        half = 1 - z if k < 2 else z
+        own_part = half_rot[half * 2 + k % 2] * (1 - 2 * z).astype(F32)
+        rotated = ((far_part + own_part) * UNIT).astype(BF16)
 
         def block(j, carry):
-            @pl.when(j < BLOCKS)
-            def _():
-                part = jnp.dot(rotated, wts[j], preferred_element_type=F32)
-                p[k, j] = part.reshape(4, 2, 8, COLS)
-                p_copy(k, j).start()
-
-            if inline:
-
-                @pl.when(j > 0)
-                def _():
-                    pass_on(k, j - 1)
-
+            part = jnp.dot(rotated, wts[j], preferred_element_type=F32)
+            p[k, j] = part.reshape(4, 2, 8, COLS)
+            p_copy(k, j).start()
             return carry
 
-        lax.fori_loop(0, BLOCKS + inline, block, 0)
+        lax.fori_loop(0, BLOCKS, block, 0)
 
     def reduce(k):
         def block(j, carry):
-            pass_on(k, j)
+            p_copy(k, j).wait_recv()
+            q[k, j] = (p[k, j, :, c] + pr[k, j]).astype(BF16)
+            for d in range(3):
+                q_copy(k, j, d).start()
             return carry
 
         lax.fori_loop(0, BLOCKS, block, 0)
-
-    def o_copy(k, j):
-        return remote(r1.at[k, j], r1r.at[k, j], o_s.at[k, j], o_r.at[k, j], far)
 
     def gather(k):
         def block(j, carry):
@@ -263,23 +278,37 @@
             lanes = slice(j * COLS, (j + 1) * COLS)
             norm_out[s, :, lanes] = (new_out[s, :, lanes].astype(F32) * factor).astype(BF16)
 
-    combine_far(0)
-    combine_twin(0)
-    combine_far(1)
-    combine_twin(1)
+    spread(0)
+    spread(1)
+    spread(2)
+    spread(3)
+
+    @pl.when(z == 1)
+    def _():
+        lax.fori_loop(0, LOCAL // 16, dequantize, 0)
+
+    loads[4].wait()
+    rotate(0)
+    zin_copies[1].start()
+    rotate(1)
+    rotate(2)
+    rotate(3)
+    receive(0)
+    spread_far()
+    spread(4)
     multiply(0)
     reduce(0)
-    combine_far(2)
-    combine_twin(2)
+    receive(1)
     multiply(1)
     reduce(1)
     gather(0)
-    combine_far(3)
-    combine_twin(3)
-    gather(1)
+    receive(2)
     multiply(2)
     reduce(2)
-    multiply(3, 1)
+    gather(1)
+    receive(3)
+    multiply(3)
+    reduce(3)
     loads[5].wait()
     gather(2)
     finish(0)
@@ -288,9 +317,10 @@
 
     for k in range(CHUNKS):
         zin_copies[k].wait_send()
-        v_copies[k].wait_send()
+    for i in range(5):
+        v_copies[i].wait_send()
         for d in range(3):
-            w_copies[k, d].wait_send()
+            w_copies[i, d].wait_send()
 
     def drain(j, carry):
         for k in range(CHUNKS):
@@ -321,10 +351,12 @@
             pltpu.VMEM((2, 8, D), BF16),
             pltpu.VMEM((LOCAL, LOCAL), BF16),
             pltpu.VMEM((BLOCKS, LOCAL, COLS), BF16),
-            pltpu.VMEM((CHUNKS, 4, 2, 8, LOCAL), F32),
-            pltpu.VMEM((CHUNKS, 4, 2, 8, LOCAL), F32),
-            pltpu.VMEM((CHUNKS, 4, 2, 8, LOCAL), BF16),
-            pltpu.VMEM((CHUNKS, 3, 4, 2, 8, LOCAL), BF16),
+            pltpu.VMEM((5, 4, 2, 8, LOCAL), BF16),
+            pltpu.VMEM((5, 4, 2, 8, LOCAL), BF16),
+            pltpu.VMEM((5, 4, 2, 8, LOCAL), BF16),
+            pltpu.VMEM((5, 3, 4, 2, 8, LOCAL), BF16),
+            pltpu.VMEM((4, 64, LOCAL), F32),
+            pltpu.VMEM((3, 4, 2, 8, LOCAL), BF16),
             pltpu.VMEM((CHUNKS, BLOCKS, 4, 2, 8, COLS), F32),
             pltpu.VMEM((CHUNKS, BLOCKS, 4, 8, COLS), F32),
             pltpu.VMEM((CHUNKS, BLOCKS, 4, 8, COLS), BF16),
@@ -337,10 +369,10 @@
             sem((CHUNKS,)),
             sem,
             sem,
-            sem((CHUNKS,)),
-            sem((CHUNKS,)),
-            sem((CHUNKS, 3)),
-            sem((CHUNKS, 3)),
+            sem((5,)),
+            sem((5,)),
+            sem((5, 3)),
+            sem((5, 3)),
             sem((CHUNKS, BLOCKS)),
             sem((CHUNKS, BLOCKS)),
             sem((CHUNKS, BLOCKS, 3)),

time: 86 us -> 82 us (0.953)
  the two profiles are of different devices: /device:TPU:71 before, /device:TPU:17 now
where the time goes in v3:
time: 82 us; the launch traced here: 81.9 us
  Pallas kernels  78.1 us (95%)
  local copies, waits for them, and re-layouts  3.14 us (4%)
    pallas_call x1, Pallas kernels, local(): pl.pallas_call(kernel, out_shape=[jax.ShapeDtypeStruct((2, 8, D), BF16)]...  78.1 us
    unnamed x2, local copies, waits for them, and re-layouts  3.14 us

profile of v3, /device:TPU:17, one launch (start us, length us, event | category | flops | bytes accessed | tf_op | source)
XLA Modules:
  0.0 81.9 jit_solution(10225452115712813071)
XLA Ops:
  0.6 78.1 %rotated_down.1 = (bf16[2,8,4096]{2,1,0:T(8,128)(2,1)}, bf16[2,8,4096]{2,1,0:T(8,128)(2,1)}) custom-call(bf16[2,4,2,2,8,896]{5,4,3,2,1,0:T(8,128)(2,1)} %bitcast.5, s32[7,128]{1,0:T(8,128)} %bitcast.9, s32[896,512]{1,0:T(8,128)} %packed.1, s32[7,4096]{1,0:T(8,128)} %scales.1, bf16[2,8,4096]{2,1,0:T(8,128)(2,1)} %bitcast.6, ...), custom_call_target="tpu_custom_call" | custom-call | tf_op jit(solution)/shard_map/rotated_down/pallas_call | solution.py:340
  78.7 1.6 %copy.10 = bf16[16,4096]{1,0:T(8,128)(2,1)} copy(bf16[16,4096]{1,0:T(8,128)(2,1)} %bitcast.8) | data formatting | bytes 262144
  80.3 1.6 %copy.11 = bf16[16,4096]{1,0:T(8,128)(2,1)} copy(bf16[16,4096]{1,0:T(8,128)(2,1)} %bitcast.7) | data formatting | bytes 262144

commit v4 on v3

--- a/solution.py
+++ b/solution.py
@@ -71,6 +71,8 @@
     vr,
     w,
     wr,
+    ub,
+    ur,
     half_rot,
     half_send,
     p,
@@ -89,6 +91,8 @@
     v_r,
     w_s,
     w_r,
+    u_s,
+    u_r,
     p_s,
     p_r,
     q_s,
@@ -167,12 +171,14 @@
     zin_copies[0].start()
 
     sets = [z * 2 + 1, (1 - z) * 2, (1 - z) * 2 + 1, z * 2]
-    v_copies, w_copies = {}, {}
+    v_copies, w_copies, u_copies = {}, {}, {}
     for i in range(5):
         source = v.at[sets[i]] if i < 4 else v.at[4]
         v_copies[i] = remote(source, vr.at[i], v_s.at[i], v_r.at[i], twin)
         for d in range(3):
-            w_copies[i, d] = remote(w.at[i], wr.at[i, d], w_s.at[i, d], w_r.at[i, d], ring[d])
+            block = w.at[i, lax.rem(y + d + 1, 4)]
+            w_copies[i, d] = remote(block, wr.at[i, d], w_s.at[i, d], w_r.at[i, d], ring[d])
+            u_copies[i, d] = remote(ub.at[i, d], ur.at[i, y], u_s.at[i, d], u_r.at[i, d], ring[d])
     for i in range(4):
         v_copies[i].start()
 
@@ -184,15 +190,24 @@
         for d in range(3):
             w_copies[i, d].start()
 
+    def turn(i):
+        parts = [w[i, y].astype(F32)]
+        for d in range(3):
+            w_copies[i, d].wait_recv()
+            parts.append(wr[i, d].astype(F32))
+        for e in (1, 2, 3, 0):
+            target = lax.rem(y + e, 4)
+            u = sum(part * sign_of(target & lax.rem(y + 4 - d, 4)) for d, part in enumerate(parts))
+            if e:
+                ub[i, e - 1] = u.astype(BF16)
+                u_copies[i, e - 1].start()
+            else:
+                ur[i, y] = u.astype(BF16)
+
     def absorb(i):
         for d in range(3):
-            w_copies[i, d].wait_recv()
-        u = w[i].astype(F32) * sign_of(y)
-        for d in range(3):
-            source = lax.rem(y + 3 - d, 4)
-            u = u + wr[i, d].astype(F32) * sign_of(y & source)
-        u = u.reshape(64, LOCAL).astype(BF16)
-        return jnp.dot(u, table[...], preferred_element_type=F32)
+            u_copies[i, d].wait_recv()
+        return jnp.dot(ur[i].reshape(64, LOCAL), table[...], preferred_element_type=F32)
 
     def rotate(i):
         mine = absorb(i)
@@ -202,8 +217,6 @@
 
     def receive(k):
         zin_copies[k].wait_recv()
-        if k + 2 < CHUNKS:
-            zin_copies[k + 2].start()
 
     def spread_far():
         sg_copy.wait()
@@ -287,26 +300,33 @@
     def _():
         lax.fori_loop(0, LOCAL // 16, dequantize, 0)
 
+    turn(0)
+    turn(1)
+    turn(2)
     loads[4].wait()
     rotate(0)
     zin_copies[1].start()
+    turn(3)
     rotate(1)
     rotate(2)
     rotate(3)
     receive(0)
+    zin_copies[2].start()
     spread_far()
     spread(4)
+    turn(4)
+    zin_copies[3].start()
     multiply(0)
     reduce(0)
     receive(1)
     multiply(1)
     reduce(1)
-    gather(0)
     receive(2)
     multiply(2)
     reduce(2)
+    gather(0)
+    receive(3)
     gather(1)
-    receive(3)
     multiply(3)
     reduce(3)
     loads[5].wait()
@@ -321,6 +341,7 @@
         v_copies[i].wait_send()
         for d in range(3):
             w_copies[i, d].wait_send()
+            u_copies[i, d].wait_send()
 
     def drain(j, carry):
         for k in range(CHUNKS):
@@ -354,7 +375,9 @@
             pltpu.VMEM((5, 4, 2, 8, LOCAL), BF16),
             pltpu.VMEM((5, 4, 2, 8, LOCAL), BF16),
             pltpu.VMEM((5, 4, 2, 8, LOCAL), BF16),
-            pltpu.VMEM((5, 3, 4, 2, 8, LOCAL), BF16),
+            pltpu.VMEM((5, 3, 2, 8, LOCAL), BF16),
+            pltpu.VMEM((5, 3, 2, 8, LOCAL), BF16),
+            pltpu.VMEM((5, 4, 2, 8, LOCAL), BF16),
             pltpu.VMEM((4, 64, LOCAL), F32),
             pltpu.VMEM((3, 4, 2, 8, LOCAL), BF16),
             pltpu.VMEM((CHUNKS, BLOCKS, 4, 2, 8, COLS), F32),
@@ -373,6 +396,8 @@
             sem((5,)),
             sem((5, 3)),
             sem((5, 3)),
+            sem((5, 3)),
+            sem((5, 3)),
             sem((CHUNKS, BLOCKS)),
             sem((CHUNKS, BLOCKS)),
             sem((CHUNKS, BLOCKS, 3)),
@@ -381,7 +406,7 @@
             sem((2, BLOCKS)),
         ],
         compiler_params=pltpu.CompilerParams(
-            collective_id=0, has_side_effects=True, vmem_limit_bytes=66500000
+            collective_id=0, has_side_effects=True, vmem_limit_bytes=56180000
         ),
         name="rotated_down",
     )(

time: 82 us -> 76.5 us (0.933)
  the two profiles are of different devices: /device:TPU:17 before, /device:TPU:120 now
where the time goes in v4:
time: 76.5 us; the launch traced here: 76.3 us
  Pallas kernels  73.7 us (96%)
  local copies, waits for them, and re-layouts  1.99 us (3%)
    pallas_call x1, Pallas kernels, local(): pl.pallas_call(kernel, out_shape=[jax.ShapeDtypeStruct((2, 8, D), BF16)]...  73.7 us
    unnamed x4, local copies, waits for them, and re-layouts  1.99 us

profile of v4, /device:TPU:120, one launch (start us, length us, event | category | flops | bytes accessed | tf_op | source)
XLA Modules:
  0.0 76.3 jit_solution(7629229159807708436)
XLA Ops:
  0.6 0.0 copy-start
  0.6 0.7 copy-done
  1.3 73.7 %rotated_down.1 = (bf16[2,8,4096]{2,1,0:T(8,128)(2,1)S(1)}, bf16[2,8,4096]{2,1,0:T(8,128)(2,1)S(1)}) custom-call(bf16[2,4,2,2,8,896]{5,4,3,2,1,0:T(8,128)(2,1)} %bitcast.8, s32[7,128]{1,0:T(8,128)S(1)} %bitcast.7, s32[896,512]{1,0:T(8,128)} %packed.1, s32[7,4096]{1,0:T(8,128)} %scales.1, bf16[2,8,4096]{2,1,0:T(8,128)(2,1)} %bitcast.9, ...), custom_call_target="tpu_custom_call" | custom-call | tf_op jit(solution)/shard_map/rotated_down/pallas_call | solution.py:361
  75.0 0.7 copy.10
  75.7 0.7 copy.11
Async XLA Ops:
  0.6 0.7 copy-start

commit v5 on v4

--- a/solution.py
+++ b/solution.py
@@ -132,6 +132,9 @@
             src_ref=src, dst_ref=dst, send_sem=ss, recv_sem=rs, device_id=peer, device_id_type=MESH
         )
 
+    def await_bytes(ref, semaphore):
+        pltpu.make_async_copy(ref, ref, semaphore).wait()
+
     def dequantize(i, carry):
         rows = pl.ds(pl.multiple_of(i * 16, 16), 16)
         words = pk[rows, :] ^ jnp.int32(-2004318072)
@@ -164,7 +167,7 @@
     sg_copy.start()
     zin_copies = [
         remote(
-            h.at[z, :, :, 0] if k == 0 else half_send.at[k - 1], zin.at[k], zin_s.at[k], zin_r.at[k], far
+            h.at[z, :, :, 0] if k == 0 else half_send.at[k - 1], zin.at[k], zin_s, zin_r.at[k], far
         )
         for k in range(CHUNKS)
     ]
@@ -174,11 +177,11 @@
     v_copies, w_copies, u_copies = {}, {}, {}
     for i in range(5):
         source = v.at[sets[i]] if i < 4 else v.at[4]
-        v_copies[i] = remote(source, vr.at[i], v_s.at[i], v_r.at[i], twin)
+        v_copies[i] = remote(source, vr.at[i], v_s, v_r.at[i], twin)
         for d in range(3):
             block = w.at[i, lax.rem(y + d + 1, 4)]
-            w_copies[i, d] = remote(block, wr.at[i, d], w_s.at[i, d], w_r.at[i, d], ring[d])
-            u_copies[i, d] = remote(ub.at[i, d], ur.at[i, y], u_s.at[i, d], u_r.at[i, d], ring[d])
+            w_copies[i, d] = remote(block, wr.at[i, d], w_s, w_r.at[i], ring[d])
+            u_copies[i, d] = remote(ub.at[i, d], ur.at[i, y], u_s, u_r.at[i], ring[d])
     for i in range(4):
         v_copies[i].start()
 
@@ -192,8 +195,8 @@
 
     def turn(i):
         parts = [w[i, y].astype(F32)]
+        await_bytes(wr.at[i], w_r.at[i])
         for d in range(3):
-            w_copies[i, d].wait_recv()
             parts.append(wr[i, d].astype(F32))
         for e in (1, 2, 3, 0):
             target = lax.rem(y + e, 4)
@@ -205,8 +208,7 @@
                 ur[i, y] = u.astype(BF16)
 
     def absorb(i):
-        for d in range(3):
-            u_copies[i, d].wait_recv()
+        await_bytes(ub.at[i], u_r.at[i])
         return jnp.dot(ur[i].reshape(64, LOCAL), table[...], preferred_element_type=F32)
 
     def rotate(i):
@@ -228,15 +230,15 @@
         v_copies[4].start()
 
     def p_copy(k, j):
-        return remote(p.at[k, j, :, 1 - c], pr.at[k, j], p_s.at[k, j], p_r.at[k, j], twin)
+        return remote(p.at[k, j, :, 1 - c], pr.at[k, j], p_s, p_r.at[k, j], twin)
 
     def q_copy(k, j, d):
         return remote(
-            q.at[k, j, lax.rem(y + d + 1, 4)], qr.at[k, j, d], q_s.at[k, j, d], q_r.at[k, j, d], ring[d]
+            q.at[k, j, lax.rem(y + d + 1, 4)], qr.at[k, j, d], q_s, q_r.at[k, j], ring[d]
         )
 
     def o_copy(k, j):
-        return remote(r1.at[k, j], r1r.at[k, j], o_s.at[k, j], o_r.at[k, j], far)
+        return remote(r1.at[k, j], r1r.at[k, j], o_s, o_r.at[k], far)
 
     def multiply(k):
         far_part = absorb(4) if k == 0 else zin[k].astype(F32).reshape(64, LOCAL)
@@ -263,16 +265,18 @@
         lax.fori_loop(0, BLOCKS, block, 0)
 
     def gather(k):
+        if k >= 2:
+            await_bytes(r1r.at[k - 2], o_r.at[k - 2])
+
         def block(j, carry):
             total = p[k, j, y, c] + pr[k, j, y]
+            await_bytes(qr.at[k, j], q_r.at[k, j])
             for d in range(3):
-                q_copy(k, j, d).wait_recv()
                 total = total + qr[k, j, d].astype(F32)
             if k < 2:
                 r1[k, j] = total.astype(BF16)
                 o_copy(k, j).start()
             else:
-                o_copy(k - 2, j).wait_recv()
                 acc[k - 2, j] = total + r1r[k - 2, j].astype(F32)
             return carry
 
@@ -322,11 +326,11 @@
     multiply(1)
     reduce(1)
     receive(2)
+    gather(0)
     multiply(2)
     reduce(2)
-    gather(0)
+    gather(1)
     receive(3)
-    gather(1)
     multiply(3)
     reduce(3)
     loads[5].wait()
@@ -334,25 +338,8 @@
     finish(0)
     gather(3)
     finish(1)
-
-    for k in range(CHUNKS):
-        zin_copies[k].wait_send()
-    for i in range(5):
-        v_copies[i].wait_send()
-        for d in range(3):
-            w_copies[i, d].wait_send()
-            u_copies[i, d].wait_send()
-
-    def drain(j, carry):
-        for k in range(CHUNKS):
-            p_copy(k, j).wait_send()
-            for d in range(3):
-                q_copy(k, j, d).wait_send()
-            if k < 2:
-                o_copy(k, j).wait_send()
-        return carry
-
-    lax.fori_loop(0, BLOCKS, drain, 0)
+    for landed, sent in ((zin, zin_s), (vr, v_s), (wr, w_s), (ub, u_s), (pr, p_s), (qr, q_s), (r1r, o_s)):
+        await_bytes(landed, sent)
 
 
 def local(hidden, signs, packed, group_scales, residual):
@@ -388,22 +375,22 @@
             pltpu.VMEM((2, BLOCKS, 8, COLS), BF16),
             pltpu.VMEM((2, BLOCKS, 8, COLS), F32),
             sem((6,)),
+            sem,
             sem((CHUNKS,)),
-            sem((CHUNKS,)),
+            sem,
             sem,
             sem,
             sem((5,)),
+            sem,
             sem((5,)),
-            sem((5, 3)),
-            sem((5, 3)),
-            sem((5, 3)),
-            sem((5, 3)),
+            sem,
+            sem((5,)),
+            sem,
             sem((CHUNKS, BLOCKS)),
+            sem,
             sem((CHUNKS, BLOCKS)),
-            sem((CHUNKS, BLOCKS, 3)),
-            sem((CHUNKS, BLOCKS, 3)),
-            sem((2, BLOCKS)),
-            sem((2, BLOCKS)),
+            sem,
+            sem((2,)),
         ],
         compiler_params=pltpu.CompilerParams(
             collective_id=0, has_side_effects=True, vmem_limit_bytes=56180000

time: 76.5 us -> 73.9 us (0.966)
  the two profiles are of different devices: /device:TPU:120 before, /device:TPU:197 now
where the time goes in v5:
time: 73.9 us; the launch traced here: 73.8 us
  Pallas kernels  71.2 us (96%)
  local copies, waits for them, and re-layouts  1.99 us (3%)
    pallas_call x1, Pallas kernels, local(): pl.pallas_call(kernel, out_shape=[jax.ShapeDtypeStruct((2, 8, D), BF16)]...  71.2 us
    unnamed x4, local copies, waits for them, and re-layouts  1.99 us

profile of v5, /device:TPU:197, one launch (start us, length us, event | category | flops | bytes accessed | tf_op | source)
XLA Modules:
  0.0 73.8 jit_solution(15442994697903380568)
XLA Ops:
  0.6 0.0 copy-start
  0.6 0.7 copy-done
  1.3 71.2 %rotated_down.1 = (bf16[2,8,4096]{2,1,0:T(8,128)(2,1)S(1)}, bf16[2,8,4096]{2,1,0:T(8,128)(2,1)S(1)}) custom-call(bf16[2,4,2,2,8,896]{5,4,3,2,1,0:T(8,128)(2,1)} %bitcast.8, s32[7,128]{1,0:T(8,128)S(1)} %bitcast.7, s32[896,512]{1,0:T(8,128)} %packed.1, s32[7,4096]{1,0:T(8,128)} %scales.1, bf16[2,8,4096]{2,1,0:T(8,128)(2,1)} %bitcast.9, ...), custom_call_target="tpu_custom_call" | custom-call | tf_op jit(solution)/shard_map/rotated_down/pallas_call | solution.py:348
  72.5 0.7 copy.10
  73.1 0.7 copy.11
Async XLA Ops:
  0.6 0.7 copy-start
